TPU v7x, 128 devices: a whole 4x4x4 slice. The times are simulated.
128 devices in a mesh: data: 1, outer: 16 (over z, y), expert: 8 (over x, core).
Axes of the slice: x: 4, y: 4, z: 4, core: 2. Of those that a mesh axis runs over, the one named last changes fastest.
Arguments:
- tokens: bfloat16 [32768, 2048], P(('data', 'outer', 'expert'))
- w_router: bfloat16 [2048, 128], replicated
- routes: int32 [32768, 8], P(('data', 'outer', 'expert'))
- w_gate: bfloat16 [128, 2048, 768], P(('outer', 'expert'))
- w_up: bfloat16 [128, 2048, 768], P(('outer', 'expert'))
- w_down: bfloat16 [128, 768, 2048], P(('outer', 'expert'))
Outputs:
- output: bfloat16 [32768, 2048], P(('data', 'outer', 'expert'))
All inputs are finite; a program needn't handle non-finite values.
Results may differ from a plain program's by a relative error of at most 0.00827862.
Values are sent between devices in bfloat16 or wider.
A program may use at most 1 GiB of HBM per device.

v0:
```python
import jax
import jax.numpy as jnp
from jax import lax
from jax.sharding import PartitionSpec as P


def local_routes(tokens, w_router, routes, num_dev, capacity):
    tok_count, top_k = routes.shape
    num_exp = w_router.shape[1]
    per_dev = num_exp // num_dev
    logits = jnp.dot(tokens, w_router, preferred_element_type=jnp.float32)
    gate_vals = jax.nn.softmax(jnp.take_along_axis(logits, routes, axis=1), axis=-1)
    flat_ids = routes.reshape(-1)
    onehot = (flat_ids[:, None] == jnp.arange(num_exp)[None, :]).astype(jnp.int32)
    slot_pos = jnp.sum((jnp.cumsum(onehot, axis=0) - onehot) * onehot, axis=1)
    total_slots = num_exp * capacity
    send_pos = (flat_ids % per_dev) * (num_dev * capacity) + (flat_ids // per_dev) * capacity + slot_pos
    dest_slot = jnp.where(slot_pos < capacity, send_pos, total_slots)
    pair_tok = jnp.arange(tok_count * top_k, dtype=jnp.int32) // top_k
    slot_tok = jnp.full((total_slots,), tok_count, jnp.int32).at[dest_slot].set(pair_tok, mode='drop')
    return gate_vals, dest_slot, slot_tok


def expert_ffn(expert_in, w_gate, w_up, w_down):
    gate_act = jnp.einsum('erd,edf->erf', expert_in, w_gate, preferred_element_type=jnp.float32)
    up_lin = jnp.einsum('erd,edf->erf', expert_in, w_up, preferred_element_type=jnp.float32)
    hidden = (jax.nn.silu(gate_act) * up_lin).astype(jnp.bfloat16)
    return jnp.einsum('erf,efd->erd', hidden, w_down, preferred_element_type=jnp.float32).astype(jnp.bfloat16)


def solution(mesh):
    outer_size = mesh.shape['outer']
    group_size = mesh.shape['expert']
    num_dev = outer_size * group_size
    row_spec = P(('data', 'outer', 'expert'), None)
    weight_spec = P(('outer', 'expert'), None, None)

    def per_device(tokens, w_router, routes, w_gate, w_up, w_down):
        tok_count, top_k = routes.shape
        model_dim = tokens.shape[1]
        num_exp = w_router.shape[1]
        per_dev = w_gate.shape[0]
        capacity = (5 * tok_count * top_k + 4 * num_exp - 1) // (4 * num_exp)
        gate_vals, dest_slot, slot_tok = local_routes(tokens, w_router, routes, num_dev, capacity)
        send_buf = jnp.take(tokens, slot_tok, axis=0, mode='fill', fill_value=0)
        send_buf = send_buf.reshape(per_dev, outer_size, group_size, capacity, model_dim)
        recv_buf = lax.all_to_all(send_buf, 'outer', 1, 1, tiled=True)
        recv_buf = lax.all_to_all(recv_buf, 'expert', 2, 2, tiled=True)
        expert_out = expert_ffn(recv_buf.reshape(per_dev, num_dev * capacity, model_dim), w_gate, w_up, w_down)
        back_buf = expert_out.reshape(per_dev, outer_size, group_size, capacity, model_dim)
        back_buf = lax.all_to_all(back_buf, 'expert', 2, 2, tiled=True)
        back_buf = lax.all_to_all(back_buf, 'outer', 1, 1, tiled=True)
        picked = jnp.take(back_buf.reshape(num_exp * capacity, model_dim), dest_slot, axis=0, mode='fill', fill_value=0)
        weighted = gate_vals[:, :, None] * picked.reshape(tok_count, top_k, model_dim).astype(jnp.float32)
        return jnp.sum(weighted, axis=1).astype(jnp.bfloat16)

    return jax.shard_map(per_device, mesh=mesh, in_specs=(row_spec, P(), row_spec, weight_spec, weight_spec, weight_spec), out_specs=row_spec, check_vma=False)
```

profile of v0, /device:TPU:32, one launch (start us, length us, event | category | flops | bytes accessed | tf_op | source)
XLA Modules:
  0.0 800.6 jit_solution(15962485115395626836)
XLA Ops:
  0.0 1.0 copy.38
  1.2 0.7 broadcast_multiply_fusion
  2.0 0.3 fusion.8
  2.4 1.0 copy-done.3
  3.4 1.3 broadcast_add_fusion
  4.7 1.3 copy.41
  6.2 1.9 fusion.7
  8.1 0.6 copy-done.6
  8.7 8.1 %scatter_custom_fusion = s32[2560]{0:T(1024)S(1)} fusion(s32[2048]{0:T(1024)S(1)} %bitcast.35, s32[2048]{0:T(1024)S(1)} %add_select_fusion, s32[]{:T(128)} %constant.97.clone.1), kind=kCustom, calls=%fused_computation.44 | custom fusion | bytes 10244 | tf_op jit(solution)/shard_map/scatter | solution.py:20
  16.8 21.6 %gather_fusion = bf16[2560,2048]{1,0:T(8,128)(2,1)} fusion(bf16[256,2048]{1,0:T(8,128)(2,1)} %param.6, s32[3072]{0:T(1024)S(1)} %pad_clamp_fusion), kind=kCustom, calls=%fused_computation | custom fusion | bytes 20981760 | tf_op jit(solution)/shard_map/jit(_take)/gather | solution.py:45
  38.3 16.4 %gather.18 = bf16[1,16,8,20,2048]{4,3,2,1,0:T(8,128)(2,1)} reshape(bf16[2560,2048]{1,0:T(8,128)(2,1)} %gather_fusion) | data formatting | bytes 20971520 | tf_op jit(solution)/shard_map/jit(_take)/gather | solution.py:45
  54.8 6.3 broadcast_select_fusion
  61.2 14.5 %copy.46 = bf16[1,16,8,20,2048]{4,2,3,0,1:T(8,128)(2,1)S(1)} copy(bf16[1,16,8,20,2048]{4,3,2,1,0:T(8,128)(2,1)S(1)} %broadcast_select_fusion) | data formatting | bytes 20971520 | tf_op jit(solution)/shard_map/jit(_take)/select_n | solution.py:45
  75.7 131.0 %all_to_all.20 = bf16[1,16,8,20,2048]{4,2,3,0,1:T(8,128)(2,1)} all-to-all(bf16[1,16,8,20,2048]{4,2,3,0,1:T(8,128)(2,1)S(1)} %copy.46), channel_id=1, replica_groups=mesh['data'=1,'outer'=16,'expert'=8] {'outer'}, dimensions={1} | all-to-all | bytes 20971520 | tf_op jit(solution)/shard_map/all_to_all | solution.py:47
  206.7 13.6 %copy.47 = bf16[1,16,8,20,2048]{4,1,3,0,2:T(8,128)(2,1)} copy(bf16[1,16,8,20,2048]{4,2,3,0,1:T(8,128)(2,1)} %all_to_all.20) | data formatting | bytes 20971520 | tf_op jit(solution)/shard_map/all_to_all | solution.py:47
  220.4 121.4 %all_to_all.21 = bf16[1,16,8,20,2048]{4,1,3,0,2:T(8,128)(2,1)S(1)} all-to-all(bf16[1,16,8,20,2048]{4,1,3,0,2:T(8,128)(2,1)} %copy.47), channel_id=1, replica_groups=mesh['data'=1,'outer'=16,'expert'=8] {'expert'}, dimensions={2} | all-to-all | bytes 20971520 | tf_op jit(solution)/shard_map/all_to_all | solution.py:48
  341.8 16.8 %copy.48 = bf16[1,16,8,20,2048]{4,3,2,1,0:T(8,128)(2,1)} copy(bf16[1,16,8,20,2048]{4,1,3,0,2:T(8,128)(2,1)S(1)} %all_to_all.21) | data formatting | bytes 20971520 | tf_op jit(solution)/shard_map/all_to_all | solution.py:48
  358.6 16.5 %reshape.157 = bf16[2560,2048]{1,0:T(8,128)(2,1)} reshape(bf16[1,16,8,20,2048]{4,3,2,1,0:T(8,128)(2,1)} %copy.48) | data formatting | bytes 20971520 | tf_op jit(solution)/shard_map/reshape.14
  375.1 13.9 %fusion.4 = f32[2560,768]{1,0:T(8,128)} fusion(bf16[2560,2048]{1,0:T(8,128)(2,1)} %reshape.157, bf16[1,2048,768]{2,1,0:T(8,128)(2,1)} %param.9), kind=kOutput, calls=%fused_computation.12 | convolution fusion | flops 8053063680 | bytes 21495808 | tf_op jit(solution)/shard_map/erd,edf->erf/dot_general | solution.py:25
  388.9 24.8 %convolution_convert_fusion = bf16[2560,2048]{1,0:T(8,128)(2,1)} fusion(f32[2560,768]{1,0:T(8,128)} %fusion.4, bf16[2560,2048]{1,0:T(8,128)(2,1)} %reshape.157, bf16[1,768,2048]{2,1,0:T(8,128)(2,1)S(1)} %copy-done, bf16[1,2048,768]{2,1,0:T(8,128)(2,1)} %param.10), kind=kOutput, calls=%fused_computation.6 | convolution fusion | flops 16123166720 | bytes 35127296 | tf_op jit(solution)/shard_map/erf,efd->erd/dot_general | solution.py:28
  413.7 16.4 %reshape.161 = bf16[1,16,8,20,2048]{4,3,2,1,0:T(8,128)(2,1)} reshape(bf16[2560,2048]{1,0:T(8,128)(2,1)} %convolution_convert_fusion) | data formatting | bytes 20971520 | tf_op jit(solution)/shard_map/reshape | solution.py:50
  430.1 10.6 %copy.49 = bf16[1,16,8,20,2048]{4,1,3,0,2:T(8,128)(2,1)S(1)} copy(bf16[1,16,8,20,2048]{4,3,2,1,0:T(8,128)(2,1)} %reshape.161) | data formatting | bytes 20971520 | tf_op jit(solution)/shard_map/reshape | solution.py:50
  440.7 120.6 %all_to_all.22 = bf16[1,16,8,20,2048]{4,1,3,0,2:T(8,128)(2,1)} all-to-all(bf16[1,16,8,20,2048]{4,1,3,0,2:T(8,128)(2,1)S(1)} %copy.49), channel_id=1, replica_groups=mesh['data'=1,'outer'=16,'expert'=8] {'expert'}, dimensions={2} | all-to-all | bytes 20971520 | tf_op jit(solution)/shard_map/all_to_all | solution.py:51
  561.3 13.8 %copy.50 = bf16[1,16,8,20,2048]{4,2,3,0,1:T(8,128)(2,1)} copy(bf16[1,16,8,20,2048]{4,1,3,0,2:T(8,128)(2,1)} %all_to_all.22) | data formatting | bytes 20971520 | tf_op jit(solution)/shard_map/all_to_all | solution.py:51
  575.1 8.7 %all-to-all-start.3 = ((bf16[1,16,8,20,2048]{4,2,3,0,1:T(8,128)(2,1)}), bf16[1,16,8,20,2048]{4,2,3,0,1:T(8,128)(2,1)}, u32[]{:S(2)}, u32[]{:S(2)}) async-start(bf16[1,16,8,20,2048]{4,2,3,0,1:T(8,128)(2,1)} %copy.50), calls=%async_computation.3 | async-start | bytes 20971520 | tf_op jit(solution)/shard_map/all_to_all | solution.py:52
  584.2 0.4 fusion.20
  584.6 13.1 %gather_fusion.2 = f32[2048]{0:T(1024)S(1)} fusion(f32[256,128]{1,0:T(8,128)S(1)} %fusion.20, s32[2048]{0:T(1024)S(1)} %reshape.179), kind=kCustom, calls=%fused_computation.2 | custom fusion | bytes 32768 | tf_op jit(solution)/shard_map/jit(take_along_axis)/gather | solution.py:12
  598.4 139.3 %all-to-all-done.3 = bf16[1,16,8,20,2048]{4,2,3,0,1:T(8,128)(2,1)} async-done(((bf16[1,16,8,20,2048]{4,2,3,0,1:T(8,128)(2,1)}), bf16[1,16,8,20,2048]{4,2,3,0,1:T(8,128)(2,1)}, u32[]{:S(2)}, u32[]{:S(2)}) %all-to-all-start.3) | async-done | bytes 10485792 | tf_op jit(solution)/shard_map/all_to_all | solution.py:52
  737.7 14.0 %copy.51 = bf16[1,16,8,20,2048]{4,3,2,1,0:T(8,128)(2,1)} copy(bf16[1,16,8,20,2048]{4,2,3,0,1:T(8,128)(2,1)} %all-to-all-done.3) | data formatting | bytes 20971520 | tf_op jit(solution)/shard_map/all_to_all | solution.py:52
  751.7 16.5 %reshape.162 = bf16[2560,2048]{1,0:T(8,128)(2,1)} reshape(bf16[1,16,8,20,2048]{4,3,2,1,0:T(8,128)(2,1)} %copy.51) | data formatting | bytes 20971520 | tf_op jit(solution)/shard_map/reshape | solution.py:53
  768.2 21.8 %gather_fusion.1 = bf16[2048,2048]{1,0:T(8,128)(2,1)} fusion(bf16[2560,2048]{1,0:T(8,128)(2,1)} %reshape.162, s32[2048]{0:T(1024)S(1)} %broadcast_clamp_fusion), kind=kCustom, calls=%fused_computation.1 | custom fusion | bytes 16785408 | tf_op jit(solution)/shard_map/jit(_take)/gather | solution.py:53
  790.0 10.3 %multiply_reduce_fusion = bf16[256,2048]{1,0:T(8,128)(2,1)} fusion(bf16[2048,2048]{1,0:T(8,128)(2,1)} %gather_fusion.1, f32[256,8]{1,0:T(8,128)S(1)} %copy.37, pred[256,8]{1,0:T(8,128)(4,1)S(1)} %copy.44), kind=kLoop, calls=%fused_computation.4 | loop fusion | flops 16252928 | bytes 9447424 | tf_op jit(solution)/shard_map/reduce_sum | solution.py:55
  (46 shorter events, 1.7 us)
Async XLA Ops:
  0.0 388.9 %copy-start = (bf16[1,768,2048]{2,1,0:T(8,128)(2,1)S(1)}, bf16[1,768,2048]{2,1,0:T(8,128)(2,1)}, u32[]{:S(2)}) copy-start(bf16[1,768,2048]{2,1,0:T(8,128)(2,1)} %param.11) | copy-start | bytes 9437188
  2.4 1.0 copy-start.3
  8.1 0.6 copy-start.6
  8.7 29.7 %copy-start.8 = (s32[2048,1]{0,1:T(1,128)}, s32[2048,1]{0,1:T(1,128)S(1)}, u32[]{:S(2)}) copy-start(s32[2048,1]{0,1:T(1,128)S(1)} %compare_select_fusion) | copy-start | bytes 24580
  575.1 8.7 %copy-start.7 = (s32[2048]{0:T(1024)S(1)}, s32[2048]{0:T(1024)}, u32[]{:S(2)}) copy-start(s32[2048]{0:T(1024)} %copy-done.6) | copy-start | bytes 24580
  575.1 8.8 %copy-start.5 = (s32[256,8]{0,1:T(8,128)S(1)}, s32[256,8]{0,1:T(8,128)}, u32[]{:S(2)}) copy-start(s32[256,8]{0,1:T(8,128)} %param.8) | copy-start | bytes 24580
  575.1 9.1 %copy-start.2 = (bf16[256,2048]{1,0:T(8,128)(2,1)S(1)}, bf16[256,2048]{1,0:T(8,128)(2,1)}, u32[]{:S(2)}) copy-start(bf16[256,2048]{1,0:T(8,128)(2,1)} %param.6) | copy-start | bytes 3145732
  575.1 9.1 %copy-start.4 = (bf16[2048,128]{1,0:T(8,128)(2,1)S(1)}, bf16[2048,128]{1,0:T(8,128)(2,1)}, u32[]{:S(2)}) copy-start(bf16[2048,128]{1,0:T(8,128)(2,1)} %param.7) | copy-start | bytes 1572868
  575.1 162.6 %all-to-all-start.3 = ((bf16[1,16,8,20,2048]{4,2,3,0,1:T(8,128)(2,1)}), bf16[1,16,8,20,2048]{4,2,3,0,1:T(8,128)(2,1)}, u32[]{:S(2)}, u32[]{:S(2)}) async-start(bf16[1,16,8,20,2048]{4,2,3,0,1:T(8,128)(2,1)} %copy.50), calls=%async_computation.3 | async-start | bytes 20971520 | tf_op jit(solution)/shard_map/all_to_all | solution.py:52
  584.6 13.7 %copy-start.9 = (s32[2048,1]{0,1:T(1,128)S(1)}, s32[2048,1]{0,1:T(1,128)}, u32[]{:S(2)}) copy-start(s32[2048,1]{0,1:T(1,128)} %copy-done.8) | copy-start | bytes 24580
  768.2 32.2 %copy-start.1 = (bf16[1,768,2048]{2,1,0:T(8,128)(2,1)S(1)}, bf16[1,768,2048]{2,1,0:T(8,128)(2,1)}, u32[]{:S(2)}) copy-start(bf16[1,768,2048]{2,1,0:T(8,128)(2,1)} %param.11) | copy-start | bytes 9437188
where the time goes:
time: 808 us; the launch traced here: 801 us
  blocking collectives  373 us (46%)
  local copies, waits for them, and re-layouts  219 us (27%)
  waiting for transfers between devices  139 us (17%)
  matrix products  39.1 us (5%)
  other arithmetic  21.1 us (3%)
  starting transfers between devices  8.67 us (1%)
    all_to_all x1, waiting for transfers between devices, per_device(): back_buf = lax.all_to_all(back_buf, 'outer', 1, 1, tiled=True)  139 us
    all_to_all x1, blocking collectives, per_device(): recv_buf = lax.all_to_all(send_buf, 'outer', 1, 1, tiled=True)  131 us
    all_to_all x1, blocking collectives, per_device(): recv_buf = lax.all_to_all(recv_buf, 'expert', 2, 2, tiled=True)  121 us
    all_to_all x1, blocking collectives, per_device(): back_buf = lax.all_to_all(back_buf, 'expert', 2, 2, tiled=True)  121 us
    gather x2, local copies, waits for them, and re-layouts, per_device(): send_buf = jnp.take(tokens, slot_tok, axis=0, mode='fill', fill_value=0)  37.9 us
    reshape x2, local copies, waits for them, and re-layouts, per_device(): expert_out.reshape(per_dev, outer_size, group_size, capacity, model_dim)  27 us
    dot_general x1, matrix products, expert_ffn(): jnp.einsum('erf,efd->erd', hidden, w_down, preferred_element_type=jnp.flo...  24.8 us
    gather x1, local copies, waits for them, and re-layouts, per_device(): jnp.take(back_buf.reshape(num_exp * capacity, model_dim), dest_slot, axis...  21.8 us
  transfers between devices with their start and end apart: 1, of which 1 were waited for; matrix products, arithmetic and copies ran while one was open for 2% of the time, Pallas kernels for 0%

commit v1 on v0

--- a/solution.py
+++ b/solution.py
@@ -1,7 +1,13 @@
+import functools
+
 import jax
 import jax.numpy as jnp
 from jax import lax
+from jax.experimental import pallas as pl
+from jax.experimental.pallas import tpu as pltpu
 from jax.sharding import PartitionSpec as P
+
+MESH = pl.DeviceIdType.MESH
 
 
 def local_routes(tokens, w_router, routes, num_dev, capacity):
@@ -28,6 +34,53 @@
     return jnp.einsum('erf,efd->erd', hidden, w_down, preferred_element_type=jnp.float32).astype(jnp.bfloat16)
 
 
+def exchange_kernel(outer_size, group_size, src, dst, send_sem, recv_sem, self_sem):
+    num_dev = outer_size * group_size
+    me = lax.axis_index('outer') * group_size + lax.axis_index('expert')
+
+    def peer(step):
+        other = lax.rem(me + step, num_dev)
+        return other, {'outer': other // group_size, 'expert': lax.rem(other, group_size)}
+
+    barrier = pltpu.get_barrier_semaphore()
+
+    def greet(step, carry):
+        pl.semaphore_signal(barrier, inc=1, device_id=peer(step)[1], device_id_type=MESH)
+        return carry
+
+    lax.fori_loop(1, num_dev, greet, 0)
+    pl.semaphore_wait(barrier, num_dev - 1)
+    own = pltpu.make_async_copy(src.at[me], dst.at[me], self_sem)
+    own.start()
+
+    def send(step, carry):
+        other, where = peer(step)
+        pltpu.make_async_remote_copy(src_ref=src.at[other], dst_ref=dst.at[me], send_sem=send_sem.at[other], recv_sem=recv_sem.at[me], device_id=where, device_id_type=MESH).start()
+        return carry
+
+    lax.fori_loop(1, num_dev, send, 0)
+
+    def finish(step, carry):
+        other, where = peer(step)
+        pltpu.make_async_remote_copy(src_ref=src.at[other], dst_ref=dst.at[other], send_sem=send_sem.at[other], recv_sem=recv_sem.at[other], device_id=where, device_id_type=MESH).wait()
+        return carry
+
+    lax.fori_loop(1, num_dev, finish, 0)
+    own.wait()
+
+
+def exchange(buf, outer_size, group_size, collective_id):
+    num_dev = outer_size * group_size
+    return pl.pallas_call(
+        functools.partial(exchange_kernel, outer_size, group_size),
+        out_shape=jax.ShapeDtypeStruct(buf.shape, buf.dtype),
+        in_specs=[pl.BlockSpec(memory_space=pl.ANY)],
+        out_specs=pl.BlockSpec(memory_space=pl.ANY),
+        scratch_shapes=[pltpu.SemaphoreType.DMA((num_dev,)), pltpu.SemaphoreType.DMA((num_dev,)), pltpu.SemaphoreType.DMA],
+        compiler_params=pltpu.CompilerParams(collective_id=collective_id, has_side_effects=True),
+    )(buf)
+
+
 def solution(mesh):
     outer_size = mesh.shape['outer']
     group_size = mesh.shape['expert']
@@ -43,13 +96,9 @@
         capacity = (5 * tok_count * top_k + 4 * num_exp - 1) // (4 * num_exp)
         gate_vals, dest_slot, slot_tok = local_routes(tokens, w_router, routes, num_dev, capacity)
         send_buf = jnp.take(tokens, slot_tok, axis=0, mode='fill', fill_value=0)
-        send_buf = send_buf.reshape(per_dev, outer_size, group_size, capacity, model_dim)
-        recv_buf = lax.all_to_all(send_buf, 'outer', 1, 1, tiled=True)
-        recv_buf = lax.all_to_all(recv_buf, 'expert', 2, 2, tiled=True)
+        recv_buf = exchange(send_buf.reshape(num_dev, capacity, model_dim), outer_size, group_size, 0)
         expert_out = expert_ffn(recv_buf.reshape(per_dev, num_dev * capacity, model_dim), w_gate, w_up, w_down)
-        back_buf = expert_out.reshape(per_dev, outer_size, group_size, capacity, model_dim)
-        back_buf = lax.all_to_all(back_buf, 'expert', 2, 2, tiled=True)
-        back_buf = lax.all_to_all(back_buf, 'outer', 1, 1, tiled=True)
+        back_buf = exchange(expert_out.reshape(num_dev, capacity, model_dim), outer_size, group_size, 1)
         picked = jnp.take(back_buf.reshape(num_exp * capacity, model_dim), dest_slot, axis=0, mode='fill', fill_value=0)
         weighted = gate_vals[:, :, None] * picked.reshape(tok_count, top_k, model_dim).astype(jnp.float32)
         return jnp.sum(weighted, axis=1).astype(jnp.bfloat16)

time: 808 us -> 683 us (0.85)
  Pallas kernels: 0 us -> 480 us
  blocking collectives: 373 us -> 0 us
  waiting for transfers between devices: 139 us -> 0 us
  local copies, waits for them, and re-layouts: 219 us -> 135 us
  starting transfers between devices: 8.67 us -> 0 us
    pallas_call x0 -> x2, Pallas kernels: none -> 480 us  [exchange(): pl.pallas_call(functools.partial(exchange_kernel, outer_size, group_size)...]
    all_to_all x3 -> x0, blocking collectives: 373 us -> none  [the longest x1 131 us: per_device(): recv_buf = lax.all_to_all(send_buf, 'outer', 1, 1, tiled=True)]
    all_to_all x1 -> x0, waiting for transfers between devices: 139 us -> none  [per_device(): back_buf = lax.all_to_all(back_buf, 'outer', 1, 1, tiled=True)]
    all_to_all x4 -> x0, local copies, waits for them, and re-layouts: 58.2 us -> none  [the longest x1 16.8 us: per_device(): recv_buf = lax.all_to_all(recv_buf, 'expert', 2, 2, tiled=True)]
    select_n x1 -> x0, local copies, waits for them, and re-layouts: 14.5 us -> none  [per_device(): send_buf = jnp.take(tokens, slot_tok, axis=0, mode='fill', fill_value=0)]
    reshape x2 -> x1, local copies, waits for them, and re-layouts: 27 us -> 16.4 us  [per_device(): expert_out.reshape(num_dev, capacity, model_dim)]
    all_to_all x1 -> x0, starting transfers between devices: 8.67 us -> none  [per_device(): back_buf = lax.all_to_all(back_buf, 'outer', 1, 1, tiled=True)]
  transfers between devices with their start and end apart: 1 -> 0, of which waited for: 1 -> 0; matrix products, arithmetic and copies ran while one was open for 2% -> 0% of each run, Pallas kernels for 0% -> 0%
where the time goes in v1:
time: 683 us; the launch traced here: 680 us
  Pallas kernels  480 us (70%)
  local copies, waits for them, and re-layouts  135 us (20%)
  matrix products  39 us (6%)
  other arithmetic  25.3 us (4%)
    pallas_call x2, Pallas kernels, exchange(): pl.pallas_call(functools.partial(exchange_kernel, outer_size, group_size)...  480 us
    gather x2, local copies, waits for them, and re-layouts, per_device(): send_buf = jnp.take(tokens, slot_tok, axis=0, mode='fill', fill_value=0)  37.9 us
    dot_general x1, matrix products, expert_ffn(): jnp.einsum('erf,efd->erd', hidden, w_down, preferred_element_type=jnp.flo...  24.8 us
    gather x1, local copies, waits for them, and re-layouts, per_device(): jnp.take(back_buf.reshape(num_exp * capacity, model_dim), dest_slot, axis...  21.8 us
    another operation x4, local copies, waits for them, and re-layouts  17.8 us
    reshape x1, local copies, waits for them, and re-layouts, per_device(): back_buf.reshape(num_exp * capacity, model_dim)  16.5 us
    reshape x1, local copies, waits for them, and re-layouts, per_device(): expert_out.reshape(num_dev, capacity, model_dim)  16.4 us
    dot_general x1, matrix products, expert_ffn(): jnp.einsum('erd,edf->erf', expert_in, w_gate, preferred_element_type=jnp....  13.9 us

profile of v1, /device:TPU:32, one launch (start us, length us, event | category | flops | bytes accessed | tf_op | source)
XLA Modules:
  0.0 679.9 jit_solution(4569169377173167841)
XLA Ops:
  0.0 1.0 copy.22
  1.0 0.1 eq.31
  1.1 0.1 copy.24
  1.2 0.3 fusion.8
  1.6 1.0 copy-done.3
  2.6 1.3 broadcast_add_fusion
  3.9 1.3 copy.25
  5.1 0.1 eq.27
  5.3 1.9 fusion.7
  7.1 0.7 broadcast_multiply_fusion
  7.8 0.1 copy.29
  8.0 0.1 mul.45
  8.1 8.2 %scatter_custom_fusion = s32[2560]{0:T(1024)S(1)} fusion(s32[2048]{0:T(1024)S(1)} %bitcast.35, s32[2048]{0:T(1024)S(1)} %add_select_fusion, s32[]{:T(128)} %constant.97.clone.1), kind=kCustom, calls=%fused_computation.44 | custom fusion | bytes 10244 | tf_op jit(solution)/shard_map/scatter | solution.py:26
  16.4 21.5 %gather_fusion = bf16[2560,2048]{1,0:T(8,128)(2,1)} fusion(bf16[256,2048]{1,0:T(8,128)(2,1)} %param.6, s32[3072]{0:T(1024)S(1)} %pad_clamp_fusion), kind=kCustom, calls=%fused_computation | custom fusion | bytes 20981760 | tf_op jit(solution)/shard_map/jit(_take)/gather | solution.py:98
  37.9 16.4 %gather.18 = bf16[128,20,2048]{2,1,0:T(8,128)(2,1)} reshape(bf16[2560,2048]{1,0:T(8,128)(2,1)} %gather_fusion) | data formatting | bytes 20971520 | tf_op jit(solution)/shard_map/jit(_take)/gather | solution.py:98
  54.3 0.1 broadcast_in_dim.41
  54.4 10.6 %broadcast_select_fusion.src = bf16[128,20,2048]{2,1,0:T(8,128)(2,1)} fusion(bf16[128,20,2048]{2,1,0:T(8,128)(2,1)} %gather.18, pred[128,20]{1,0:T(8,128)(4,1)S(1)} %broadcast_in_dim.41), kind=kLoop, calls=%fused_computation.5 | loop fusion | flops 5242880 | bytes 20974080 | tf_op jit(solution)/shard_map/jit(_take)/select_n | solution.py:98
  65.0 222.0 %shard_map.64 = bf16[128,20,2048]{2,1,0:T(8,128)(2,1)} custom-call(bf16[128,20,2048]{2,1,0:T(8,128)(2,1)} %broadcast_select_fusion.src), custom_call_target="tpu_custom_call" | custom-call | tf_op jit(solution)/shard_map/pallas_call | solution.py:74
  287.0 16.5 %reshape.146 = bf16[2560,2048]{1,0:T(8,128)(2,1)} reshape(bf16[128,20,2048]{2,1,0:T(8,128)(2,1)} %shard_map.64) | data formatting | bytes 20971520 | tf_op jit(solution)/shard_map/reshape.14
  303.5 13.9 %fusion.4 = f32[2560,768]{1,0:T(8,128)} fusion(bf16[2560,2048]{1,0:T(8,128)(2,1)} %reshape.146, bf16[1,2048,768]{2,1,0:T(8,128)(2,1)} %param.9), kind=kOutput, calls=%fused_computation.12 | convolution fusion | flops 8053063680 | bytes 21495808 | tf_op jit(solution)/shard_map/erd,edf->erf/dot_general | solution.py:31
  317.3 24.8 %convolution_convert_fusion = bf16[2560,2048]{1,0:T(8,128)(2,1)} fusion(f32[2560,768]{1,0:T(8,128)} %fusion.4, bf16[2560,2048]{1,0:T(8,128)(2,1)} %reshape.146, bf16[1,768,2048]{2,1,0:T(8,128)(2,1)S(1)} %copy-done, bf16[1,2048,768]{2,1,0:T(8,128)(2,1)} %param.10), kind=kOutput, calls=%fused_computation.6 | convolution fusion | flops 16123166720 | bytes 35127296 | tf_op jit(solution)/shard_map/erf,efd->erd/dot_general | solution.py:34
  342.1 16.4 %reshape.150.src = bf16[128,20,2048]{2,1,0:T(8,128)(2,1)} reshape(bf16[2560,2048]{1,0:T(8,128)(2,1)} %convolution_convert_fusion) | data formatting | bytes 20971520 | tf_op jit(solution)/shard_map/reshape | solution.py:101
  358.5 258.2 %shard_map.65 = bf16[128,20,2048]{2,1,0:T(8,128)(2,1)} custom-call(bf16[128,20,2048]{2,1,0:T(8,128)(2,1)} %reshape.150.src), custom_call_target="tpu_custom_call" | custom-call | tf_op jit(solution)/shard_map/pallas_call | solution.py:74
  616.7 16.5 %reshape.151 = bf16[2560,2048]{1,0:T(8,128)(2,1)} reshape(bf16[128,20,2048]{2,1,0:T(8,128)(2,1)} %shard_map.65) | data formatting | bytes 20971520 | tf_op jit(solution)/shard_map/reshape | solution.py:102
  633.2 21.8 %gather_fusion.1 = bf16[2048,2048]{1,0:T(8,128)(2,1)} fusion(bf16[2560,2048]{1,0:T(8,128)(2,1)} %reshape.151, s32[2048]{0:T(1024)S(1)} %broadcast_clamp_fusion), kind=kCustom, calls=%fused_computation.1 | custom fusion | bytes 16785408 | tf_op jit(solution)/shard_map/jit(_take)/gather | solution.py:102
  655.0 0.1 copy.19
  655.2 0.1 reshape.168
  655.3 0.4 fusion.20
  655.7 13.1 %gather_fusion.2 = f32[2048]{0:T(1024)S(1)} fusion(f32[256,128]{1,0:T(8,128)S(1)} %fusion.20, s32[2048]{0:T(1024)S(1)} %reshape.168), kind=kCustom, calls=%fused_computation.2 | custom fusion | bytes 32768 | tf_op jit(solution)/shard_map/jit(take_along_axis)/gather | solution.py:18
  669.1 0.1 copy.21
  669.4 0.2 copy.28
  669.6 10.3 %multiply_reduce_fusion = bf16[256,2048]{1,0:T(8,128)(2,1)} fusion(bf16[2048,2048]{1,0:T(8,128)(2,1)} %gather_fusion.1, f32[256,8]{1,0:T(8,128)S(1)} %copy.21, pred[256,8]{1,0:T(8,128)(4,1)S(1)} %copy.28), kind=kLoop, calls=%fused_computation.4 | loop fusion | flops 16252928 | bytes 9447424 | tf_op jit(solution)/shard_map/reduce_sum | solution.py:104
  (33 shorter events, 0.5 us)
Async XLA Ops:
  0.0 317.3 %copy-start = (bf16[1,768,2048]{2,1,0:T(8,128)(2,1)S(1)}, bf16[1,768,2048]{2,1,0:T(8,128)(2,1)}, u32[]{:S(2)}) copy-start(bf16[1,768,2048]{2,1,0:T(8,128)(2,1)} %param.11) | copy-start | bytes 9437188
  1.5 1.0 copy-start.3
  7.1 30.8 %copy-start.6 = (s32[2048]{0:T(1024)}, s32[2048]{0:T(1024)S(1)}, u32[]{:S(2)}) copy-start(s32[2048]{0:T(1024)S(1)} %fusion.7) | copy-start | bytes 24580
  633.2 21.8 %copy-start.5 = (s32[256,8]{0,1:T(8,128)S(1)}, s32[256,8]{0,1:T(8,128)}, u32[]{:S(2)}) copy-start(s32[256,8]{0,1:T(8,128)} %param.8) | copy-start | bytes 24580
  633.2 22.1 %copy-start.2 = (bf16[256,2048]{1,0:T(8,128)(2,1)S(1)}, bf16[256,2048]{1,0:T(8,128)(2,1)}, u32[]{:S(2)}) copy-start(bf16[256,2048]{1,0:T(8,128)(2,1)} %param.6) | copy-start | bytes 3145732
  633.2 22.1 %copy-start.4 = (bf16[2048,128]{1,0:T(8,128)(2,1)S(1)}, bf16[2048,128]{1,0:T(8,128)(2,1)}, u32[]{:S(2)}) copy-start(bf16[2048,128]{1,0:T(8,128)(2,1)} %param.7) | copy-start | bytes 1572868
  655.7 13.5 %copy-start.7 = (s32[2048]{0:T(1024)S(1)}, s32[2048]{0:T(1024)}, u32[]{:S(2)}) copy-start(s32[2048]{0:T(1024)} %copy-done.6) | copy-start | bytes 24580
  655.7 24.2 %copy-start.1 = (bf16[1,768,2048]{2,1,0:T(8,128)(2,1)S(1)}, bf16[1,768,2048]{2,1,0:T(8,128)(2,1)}, u32[]{:S(2)}) copy-start(bf16[1,768,2048]{2,1,0:T(8,128)(2,1)} %param.11) | copy-start | bytes 9437188

commit v2 on v0

v2 whole, which is shorter than its diff:
```python
import functools

import jax
import jax.numpy as jnp
from jax import lax
from jax.experimental import pallas as pl
from jax.experimental.pallas import tpu as pltpu
from jax.sharding import PartitionSpec as P

MESH = pl.DeviceIdType.MESH
BF16 = jnp.bfloat16
F32 = jnp.float32
NUM_DEV = 128
STRIDE = 37
GROUP = 8
NUM_GROUPS = NUM_DEV // GROUP
CAPACITY = 20
HEAD = 16
TAIL = CAPACITY - HEAD
PARTS = HEAD // TAIL
AHEAD = 4
BEHIND = 8


def iota(shape, dim):
    return lax.broadcasted_iota(jnp.int32, shape, dim)


def dot(a, b, dims=((1,), (0,))):
    return lax.dot_general(a, b, (dims, ((), ())), preferred_element_type=F32)


def moe_kernel(tokens, router, routes, gate_hbm, up_hbm, down_hbm, out, send, recv, back, w_gate, w_up, w_down, acc, place, gates, rows, hidden, tail_acc, weight_sem, send_sem, recv_sem, ret_sem, back_sem):
    tok_count, dim = tokens.shape
    num_exp = router.shape[1]
    top_k = routes.shape[1]
    part = dim // PARTS
    block = GROUP * HEAD
    outer = lax.axis_index('outer')
    line = lax.axis_index('expert')
    at_z, at_y = outer // 4, lax.rem(outer, 4)
    at_x, at_c = line // 2, lax.rem(line, 2)

    def peer(k, sign):
        m = lax.rem(k * STRIDE, NUM_DEV)
        to_z = lax.rem(at_z + 4 + sign * (m // 32), 4)
        to_y = lax.rem(at_y + 4 + sign * lax.rem(m // 8, 4), 4)
        to_x = lax.rem(at_x + 4 + sign * lax.rem(m // 2, 4), 4)
        to_c = lax.rem(at_c + 2 + sign * lax.rem(m, 2), 2)
        return {'outer': to_z * 4 + to_y, 'expert': to_x * 2 + to_c}

    def expert_of(k):
        m = (k * STRIDE) & (NUM_DEV - 1)
        to_z = (at_z + (m >> 5)) & 3
        to_y = (at_y + ((m >> 3) & 3)) & 3
        to_x = (at_x + ((m >> 1) & 3)) & 3
        to_c = (at_c + (m & 1)) & 1
        return to_z * 32 + to_y * 8 + to_x * 2 + to_c

    def dispatch(k, sign=1):
        return pltpu.make_async_remote_copy(src_ref=send.at[k], dst_ref=recv.at[k], send_sem=send_sem.at[k], recv_sem=recv_sem.at[k], device_id=peer(k, sign), device_id_type=MESH)

    def give_back(k, sign=-1):
        return pltpu.make_async_remote_copy(src_ref=recv.at[k], dst_ref=back.at[k], send_sem=ret_sem.at[k], recv_sem=back_sem.at[k], device_id=peer(k, sign), device_id_type=MESH)

    def each(group, what):
        def step(k, carry):
            what(k)
            return carry

        lax.fori_loop(lax.max(group * GROUP, 1), group * GROUP + GROUP, step, 0)

    barrier = pltpu.get_barrier_semaphore()

    def greet(k, carry):
        pl.semaphore_signal(barrier, inc=1, device_id=peer(k, 1), device_id_type=MESH)
        return carry

    lax.fori_loop(1, NUM_DEV, greet, 0)
    weights = [pltpu.make_async_copy(src, dst, weight_sem.at[n]) for n, (src, dst) in enumerate(((gate_hbm, w_gate), (up_hbm, w_up), (down_hbm, w_down)))]
    for copy in weights:
        copy.start()

    lanes = iota((tok_count, num_exp), 1)
    chosen = routes[:, 0:1] == lanes
    for j in range(1, top_k):
        chosen = chosen | (routes[:, j : j + 1] == lanes)
    earlier = (iota((tok_count, tok_count), 1) < iota((tok_count, tok_count), 0)).astype(F32).astype(BF16)
    count = dot(earlier, chosen.astype(F32).astype(BF16))
    place[...] = jnp.where(chosen, count, -1.0).astype(BF16)
    acc[...] = jnp.zeros_like(acc)
    pl.semaphore_wait(barrier, NUM_DEV - 1)

    def build(g):
        base = g * GROUP
        r = iota((block, num_exp), 0)
        pick = (expert_of(base + (r >> 4)) == iota((block, num_exp), 1)).astype(F32).astype(BF16)
        slots = dot(pick, place[...], ((1,), (1,)))
        r = iota((block, tok_count), 0)
        head = (slots == (r & (HEAD - 1)).astype(F32)).astype(F32).astype(BF16)
        in_tail = slots == (HEAD + (r & (TAIL - 1))).astype(F32)
        which = (r & (HEAD - 1)) >> 2
        tail_acc[...] = jnp.zeros_like(tail_acc)

        def column(q, carry):
            cols = pl.ds(pl.multiple_of(q * part, part), part)
            toks = tokens[:, cols]
            send[pl.ds(base, GROUP), :, cols] = dot(head, toks).astype(BF16).reshape(GROUP, HEAD, part)
            tail = jnp.where(in_tail & (which == q), 1.0, 0.0).astype(BF16)
            tail_acc[...] += dot(tail, toks)
            return carry

        lax.fori_loop(0, PARTS, column, 0)
        send[pl.ds(base, GROUP), :, dim:] = tail_acc[...].astype(BF16).reshape(GROUP, HEAD, part)

        @pl.when(g == 0)
        def _():
            recv[0] = send[0]

        each(g, lambda k: dispatch(k).start())

    def find_gates():
        lanes_chosen = place[...].astype(F32) >= 0.0
        logits = dot(tokens[...], router[...])
        top = jnp.max(jnp.where(lanes_chosen, logits, -3.0e38), axis=1, keepdims=True)
        weight = jnp.where(lanes_chosen, jnp.exp(jnp.where(lanes_chosen, logits - top, 0.0)), 0.0)
        rest = weight / jnp.sum(weight, axis=1, keepdims=True)
        for n in range(3):
            term = rest.astype(BF16)
            gates[n] = term
            rest = rest - term.astype(F32)

    def run_expert(g):
        base = g * GROUP
        each(g, lambda k: dispatch(k, -1).wait_recv())
        rows[0:block, :] = recv[pl.ds(base, GROUP), :, 0:dim].reshape(block, dim)
        tails = recv[pl.ds(base, GROUP), :, dim:].reshape(block, part)
        few = GROUP * TAIL
        i, l = iota((few, block), 0), iota((few, block), 1)
        for q in range(PARTS):
            take = (l == (i >> 2) * HEAD + q * TAIL + (i & (TAIL - 1))).astype(F32).astype(BF16)
            rows[block : block + few, q * part : (q + 1) * part] = dot(take, tails).astype(BF16)

        def up_column(n, carry):
            cols = pl.ds(pl.multiple_of(n * 256, 256), 256)
            gate = dot(rows[...], w_gate[:, cols])
            lin = dot(rows[...], w_up[:, cols])
            hidden[:, cols] = (jax.nn.silu(gate) * lin).astype(BF16)
            return carry

        lax.fori_loop(0, w_gate.shape[1] // 256, up_column, 0)
        tail_acc[...] = jnp.zeros_like(tail_acc)
        l, i = iota((block, few), 0), iota((block, few), 1)

        def down_column(q, carry):
            cols = pl.ds(pl.multiple_of(q * part, part), part)
            result = dot(hidden[...], w_down[:, cols]).astype(BF16)
            recv[pl.ds(base, GROUP), :, cols] = result[0:block].reshape(GROUP, HEAD, part)
            put = (l == (i >> 2) * HEAD + q * TAIL + (i & (TAIL - 1))).astype(F32).astype(BF16)
            tail_acc[...] += dot(put, result[block:])
            return carry

        lax.fori_loop(0, PARTS, down_column, 0)
        recv[pl.ds(base, GROUP), :, dim:] = tail_acc[...].astype(BF16).reshape(GROUP, HEAD, part)

        @pl.when(g == 0)
        def _():
            back[0] = recv[0]

        each(g, lambda k: give_back(k).start())

    def combine(g):
        base = g * GROUP
        each(g, lambda k: give_back(k, 1).wait_recv())
        l = iota((num_exp, block), 1)
        pick = (expert_of(base + (l >> 4)) == iota((num_exp, block), 0)).astype(F32).astype(BF16)
        slots = dot(place[...], pick)
        l = iota((tok_count, block), 1)
        in_head = slots == (l & (HEAD - 1)).astype(F32)
        in_tail = slots == (HEAD + (l & (TAIL - 1))).astype(F32)
        which = (l & (HEAD - 1)) >> 2
        spread = [dot(gates[n], pick) for n in range(3)]
        heads = jnp.concatenate([jnp.where(in_head, s, 0.0).astype(BF16) for s in spread], axis=0)
        tails = jnp.concatenate([jnp.where(in_tail, s, 0.0).astype(BF16) for s in spread], axis=0)
        which = jnp.concatenate([which] * 3, axis=0)

        def column(q, carry):
            cols = pl.ds(pl.multiple_of(q * part, part), part)
            total = dot(heads, back[pl.ds(base, GROUP), :, cols].reshape(block, part))
            mine = jnp.where(which == q, tails.astype(F32), 0.0).astype(BF16)
            total += dot(mine, back[pl.ds(base, GROUP), :, dim:].reshape(block, part))
            acc[:, cols] += total[0:tok_count] + (total[tok_count : 2 * tok_count] + total[2 * tok_count :])
            return carry

        lax.fori_loop(0, PARTS, column, 0)

    def step(i, carry):
        @pl.when(i < NUM_GROUPS)
        def _():
            @pl.when(i >= AHEAD)
            def _():
                each(i - AHEAD, lambda k: dispatch(k).wait_send())

            build(i)

        @pl.when(i == 2)
        def _():
            find_gates()

        @pl.when(i == AHEAD)
        def _():
            for copy in weights:
                copy.wait()

        @pl.when((i >= AHEAD) & (i < NUM_GROUPS + AHEAD))
        def _():
            run_expert(i - AHEAD)

        @pl.when(i >= BEHIND)
        def _():
            combine(i - BEHIND)

        return carry

    lax.fori_loop(0, NUM_GROUPS + BEHIND, step, 0)
    out[...] = acc[...].astype(BF16)

    def drain(k, carry):
        give_back(k).wait_send()
        return carry

    lax.fori_loop(1, NUM_DEV, drain, 0)

    def drain_send(k, carry):
        dispatch(k).wait_send()
        return carry

    lax.fori_loop((NUM_GROUPS - AHEAD) * GROUP, NUM_DEV, drain_send, 0)


def solution(mesh):
    row_spec = P(('data', 'outer', 'expert'), None)
    weight_spec = P(('outer', 'expert'), None, None)

    def per_device(tokens, w_router, routes, w_gate, w_up, w_down):
        tok_count, dim = tokens.shape
        num_exp = w_router.shape[1]
        ff = w_gate.shape[2]
        width = dim + dim // PARTS
        few = GROUP * CAPACITY
        vmem = pl.BlockSpec(memory_space=pltpu.VMEM)
        hbm = pl.BlockSpec(memory_space=pl.ANY)
        dma = pltpu.SemaphoreType.DMA
        return pl.pallas_call(
            moe_kernel,
            out_shape=jax.ShapeDtypeStruct((tok_count, dim), BF16),
            in_specs=[vmem, vmem, vmem, hbm, hbm, hbm],
            out_specs=vmem,
            scratch_shapes=[
                pltpu.VMEM((NUM_DEV, HEAD, width), BF16),
                pltpu.VMEM((NUM_DEV, HEAD, width), BF16),
                pltpu.VMEM((NUM_DEV, HEAD, width), BF16),
                pltpu.VMEM((dim, ff), BF16),
                pltpu.VMEM((dim, ff), BF16),
                pltpu.VMEM((ff, dim), BF16),
                pltpu.VMEM((tok_count, dim), F32),
                pltpu.VMEM((tok_count, num_exp), BF16),
                pltpu.VMEM((3, tok_count, num_exp), BF16),
                pltpu.VMEM((few, dim), BF16),
                pltpu.VMEM((few, ff), BF16),
                pltpu.VMEM((GROUP * HEAD, dim // PARTS), F32),
                dma((3,)),
                dma((NUM_DEV,)),
                dma((NUM_DEV,)),
                dma((NUM_DEV,)),
                dma((NUM_DEV,)),
            ],
            compiler_params=pltpu.CompilerParams(collective_id=0, has_side_effects=True, vmem_limit_bytes=63 * 2**20),
        )(tokens, w_router, routes, w_gate[0], w_up[0], w_down[0])

    return jax.shard_map(per_device, mesh=mesh, in_specs=(row_spec, P(), row_spec, weight_spec, weight_spec, weight_spec), out_specs=row_spec, check_vma=False)
```

time: 808 us -> 353 us (0.44)
  the two profiles are of different devices: /device:TPU:32 before, /device:TPU:21 now
where the time goes in v2:
time: 353 us
  Pallas kernels  349 us (99%)
  local copies, waits for them, and re-layouts  3.79 us (1%)
    pallas_call x1, Pallas kernels, per_device(): pl.pallas_call(moe_kernel, out_shape=jax.ShapeDtypeStruct((tok_count, dim...  349 us

profile of v2, /device:TPU:21, one launch (start us, length us, event | category | flops | bytes accessed | tf_op | source)
XLA Modules:
  0.0 353.2 jit_solution(14999536511586020254)
XLA Ops:
  0.0 1.5 copy.7.routes
  1.5 349.4 %shard_map.64 = bf16[256,2048]{1,0:T(8,128)(2,1)} custom-call(bf16[256,2048]{1,0:T(8,128)(2,1)} %tokens.1, bf16[2048,128]{1,0:T(8,128)(2,1)} %router.1, s32[256,8]{1,0:T(8,128)} %copy.7.routes, bf16[2048,768]{1,0:T(8,128)(2,1)} %bitcast.3, bf16[2048,768]{1,0:T(8,128)(2,1)} %bitcast.4, bf16[768,2048]{1,0:T(8,128)(2,1)} %bitcast.5), custom_call_target="tpu_custom_call" | custom-call | tf_op jit(solution)/shard_map/pallas_call | solution.py:254
  350.9 2.3 copy.9

commit v3 on v2

--- a/solution.py
+++ b/solution.py
@@ -12,6 +12,8 @@
 F32 = jnp.float32
 NUM_DEV = 128
 STRIDE = 37
+MIX = 1
+FLIP = 1
 GROUP = 8
 NUM_GROUPS = NUM_DEV // GROUP
 CAPACITY = 20
@@ -30,10 +32,10 @@
     return lax.dot_general(a, b, (dims, ((), ())), preferred_element_type=F32)
 
 
-def moe_kernel(tokens, router, routes, gate_hbm, up_hbm, down_hbm, out, send, recv, back, w_gate, w_up, w_down, acc, place, gates, rows, hidden, tail_acc, weight_sem, send_sem, recv_sem, ret_sem, back_sem):
+def moe_kernel(tokens, router, routes, gate_hbm, up_hbm, down_hbm, out, send, recv, back, w_gate, w_up, w_down, acc, place_t, place, gates, rows, hidden, tail_acc, ready, weight_sem, send_sem, recv_sem, ret_sem, back_sem):
     tok_count, dim = tokens.shape
     num_exp = router.shape[1]
-    top_k = routes.shape[1]
+    top_k = routes.shape[0]
     part = dim // PARTS
     block = GROUP * HEAD
     outer = lax.axis_index('outer')
@@ -43,18 +45,24 @@
 
     def peer(k, sign):
         m = lax.rem(k * STRIDE, NUM_DEV)
-        to_z = lax.rem(at_z + 4 + sign * (m // 32), 4)
-        to_y = lax.rem(at_y + 4 + sign * lax.rem(m // 8, 4), 4)
-        to_x = lax.rem(at_x + 4 + sign * lax.rem(m // 2, 4), 4)
-        to_c = lax.rem(at_c + 2 + sign * lax.rem(m, 2), 2)
+        to_c = lax.rem(at_c + m, 2)
+        turn = sign * (1 - 2 * FLIP * (at_c if sign > 0 else to_c))
+        shift_x = lax.rem(m // 2, 4)
+        shift_y = lax.rem(m // 8 + MIX * shift_x, 4)
+        shift_z = lax.rem(m // 32 + MIX * shift_x, 4)
+        to_z = lax.rem(at_z + 4 + turn * shift_z, 4)
+        to_y = lax.rem(at_y + 4 + turn * shift_y, 4)
+        to_x = lax.rem(at_x + 4 + turn * shift_x, 4)
         return {'outer': to_z * 4 + to_y, 'expert': to_x * 2 + to_c}
 
     def expert_of(k):
         m = (k * STRIDE) & (NUM_DEV - 1)
-        to_z = (at_z + (m >> 5)) & 3
-        to_y = (at_y + ((m >> 3) & 3)) & 3
-        to_x = (at_x + ((m >> 1) & 3)) & 3
-        to_c = (at_c + (m & 1)) & 1
+        turn = 1 - 2 * FLIP * at_c
+        shift_x = (m >> 1) & 3
+        to_z = (at_z + turn * ((m >> 5) + MIX * shift_x)) & 3
+        to_y = (at_y + turn * ((m >> 3) + MIX * shift_x)) & 3
+        to_x = (at_x + turn * shift_x) & 3
+        to_c = (at_c + m) & 1
         return to_z * 32 + to_y * 8 + to_x * 2 + to_c
 
     def dispatch(k, sign=1):
@@ -70,32 +78,38 @@
 
         lax.fori_loop(lax.max(group * GROUP, 1), group * GROUP + GROUP, step, 0)
 
+    lines = lax.axis_size('expert')
+    outers = lax.axis_size('outer')
     barrier = pltpu.get_barrier_semaphore()
 
-    def greet(k, carry):
-        pl.semaphore_signal(barrier, inc=1, device_id=peer(k, 1), device_id_type=MESH)
-        return carry
-
-    lax.fori_loop(1, NUM_DEV, greet, 0)
+    def in_line(n):
+        return {'outer': outer, 'expert': lax.rem(line + n, lines)}
+
+    for n in range(1, lines):
+        pl.semaphore_signal(barrier, inc=1, device_id=in_line(n), device_id_type=MESH)
+    for n in range(1, outers):
+        pl.semaphore_signal(barrier, inc=1, device_id={'outer': lax.rem(outer + n, outers), 'expert': line}, device_id_type=MESH)
     weights = [pltpu.make_async_copy(src, dst, weight_sem.at[n]) for n, (src, dst) in enumerate(((gate_hbm, w_gate), (up_hbm, w_up), (down_hbm, w_down)))]
     for copy in weights:
         copy.start()
 
-    lanes = iota((tok_count, num_exp), 1)
-    chosen = routes[:, 0:1] == lanes
+    kinds = iota((num_exp, tok_count), 0)
+    chosen = routes[0:1, :] == kinds
     for j in range(1, top_k):
-        chosen = chosen | (routes[:, j : j + 1] == lanes)
-    earlier = (iota((tok_count, tok_count), 1) < iota((tok_count, tok_count), 0)).astype(F32).astype(BF16)
-    count = dot(earlier, chosen.astype(F32).astype(BF16))
-    place[...] = jnp.where(chosen, count, -1.0).astype(BF16)
-    acc[...] = jnp.zeros_like(acc)
-    pl.semaphore_wait(barrier, NUM_DEV - 1)
+        chosen = chosen | (routes[j : j + 1, :] == kinds)
+    square = (tok_count, tok_count)
+    earlier = (iota(square, 0) < iota(square, 1)).astype(F32).astype(BF16)
+    count = dot(chosen.astype(F32).astype(BF16), earlier)
+    place_t[...] = jnp.where(chosen, count, -1.0).astype(BF16)
+    pl.semaphore_wait(barrier, lines + outers - 2)
+    for n in range(1, lines):
+        pl.semaphore_signal(ready, inc=1, device_id=in_line(n), device_id_type=MESH)
 
     def build(g):
         base = g * GROUP
         r = iota((block, num_exp), 0)
         pick = (expert_of(base + (r >> 4)) == iota((block, num_exp), 1)).astype(F32).astype(BF16)
-        slots = dot(pick, place[...], ((1,), (1,)))
+        slots = dot(pick, place_t[...])
         r = iota((block, tok_count), 0)
         head = (slots == (r & (HEAD - 1)).astype(F32)).astype(F32).astype(BF16)
         in_tail = slots == (HEAD + (r & (TAIL - 1))).astype(F32)
@@ -113,13 +127,13 @@
         lax.fori_loop(0, PARTS, column, 0)
         send[pl.ds(base, GROUP), :, dim:] = tail_acc[...].astype(BF16).reshape(GROUP, HEAD, part)
 
-        @pl.when(g == 0)
-        def _():
-            recv[0] = send[0]
-
+    def start_group(g):
         each(g, lambda k: dispatch(k).start())
 
     def find_gates():
+        same = (iota(square, 0) == iota(square, 1)).astype(F32).astype(BF16)
+        place[...] = dot(same, place_t[...], ((1,), (1,))).astype(BF16)
+        acc[...] = jnp.zeros_like(acc)
         lanes_chosen = place[...].astype(F32) >= 0.0
         logits = dot(tokens[...], router[...])
         top = jnp.max(jnp.where(lanes_chosen, logits, -3.0e38), axis=1, keepdims=True)
@@ -171,7 +185,6 @@
 
     def combine(g):
         base = g * GROUP
-        each(g, lambda k: give_back(k, 1).wait_recv())
         l = iota((num_exp, block), 1)
         pick = (expert_of(base + (l >> 4)) == iota((num_exp, block), 0)).astype(F32).astype(BF16)
         slots = dot(place[...], pick)
@@ -183,6 +196,7 @@
         heads = jnp.concatenate([jnp.where(in_head, s, 0.0).astype(BF16) for s in spread], axis=0)
         tails = jnp.concatenate([jnp.where(in_tail, s, 0.0).astype(BF16) for s in spread], axis=0)
         which = jnp.concatenate([which] * 3, axis=0)
+        each(g, lambda k: give_back(k, 1).wait_recv())
 
         def column(q, carry):
             cols = pl.ds(pl.multiple_of(q * part, part), part)
@@ -194,14 +208,20 @@
 
         lax.fori_loop(0, PARTS, column, 0)
 
+    build(0)
+    recv[0] = send[0]
+    pl.semaphore_wait(ready, lines - 1)
+    start_group(0)
+
     def step(i, carry):
-        @pl.when(i < NUM_GROUPS)
+        @pl.when((i > 0) & (i < NUM_GROUPS))
         def _():
             @pl.when(i >= AHEAD)
             def _():
                 each(i - AHEAD, lambda k: dispatch(k).wait_send())
 
             build(i)
+            start_group(i)
 
         @pl.when(i == 2)
         def _():
@@ -264,11 +284,13 @@
                 pltpu.VMEM((dim, ff), BF16),
                 pltpu.VMEM((ff, dim), BF16),
                 pltpu.VMEM((tok_count, dim), F32),
+                pltpu.VMEM((num_exp, tok_count), BF16),
                 pltpu.VMEM((tok_count, num_exp), BF16),
                 pltpu.VMEM((3, tok_count, num_exp), BF16),
                 pltpu.VMEM((few, dim), BF16),
                 pltpu.VMEM((few, ff), BF16),
                 pltpu.VMEM((GROUP * HEAD, dim // PARTS), F32),
+                pltpu.SemaphoreType.REGULAR,
                 dma((3,)),
                 dma((NUM_DEV,)),
                 dma((NUM_DEV,)),
@@ -276,6 +298,6 @@
                 dma((NUM_DEV,)),
             ],
             compiler_params=pltpu.CompilerParams(collective_id=0, has_side_effects=True, vmem_limit_bytes=63 * 2**20),
-        )(tokens, w_router, routes, w_gate[0], w_up[0], w_down[0])
+        )(tokens, w_router, routes.T, w_gate[0], w_up[0], w_down[0])
 
     return jax.shard_map(per_device, mesh=mesh, in_specs=(row_spec, P(), row_spec, weight_spec, weight_spec, weight_spec), out_specs=row_spec, check_vma=False)

time: 353 us -> 303 us (0.86)
  the two profiles are of different devices: /device:TPU:21 before, /device:TPU:0 now
where the time goes in v3:
time: 303 us
  Pallas kernels  300 us (99%)
    pallas_call x1, Pallas kernels, per_device(): pl.pallas_call(moe_kernel, out_shape=jax.ShapeDtypeStruct((tok_count, dim...  300 us

profile of v3, /device:TPU:0, one launch (start us, length us, event | category | flops | bytes accessed | tf_op | source)
XLA Modules:
  0.0 302.7 jit_solution(13128897063191232504)
XLA Ops:
  0.0 300.4 %shard_map.64 = bf16[256,2048]{1,0:T(8,128)(2,1)} custom-call(bf16[256,2048]{1,0:T(8,128)(2,1)} %tokens.1, bf16[2048,128]{1,0:T(8,128)(2,1)} %router.1, s32[8,256]{1,0:T(8,128)} %bitcast.7, bf16[2048,768]{1,0:T(8,128)(2,1)} %bitcast.4, bf16[2048,768]{1,0:T(8,128)(2,1)} %bitcast.5, bf16[768,2048]{1,0:T(8,128)(2,1)} %bitcast.6), custom_call_target="tpu_custom_call" | custom-call | tf_op jit(solution)/shard_map/pallas_call | solution.py:274
  300.4 2.3 copy.8

commit v4 on v3

--- a/solution.py
+++ b/solution.py
@@ -11,18 +11,17 @@
 BF16 = jnp.bfloat16
 F32 = jnp.float32
 NUM_DEV = 128
-STRIDE = 37
-MIX = 1
-FLIP = 1
+SHIFTS = (0, 1, 4, 3, 12, 5, 15, 2, 8, 7, 13, 6, 9, 14, 11, 10)
 GROUP = 8
 NUM_GROUPS = NUM_DEV // GROUP
 CAPACITY = 20
 HEAD = 16
 TAIL = CAPACITY - HEAD
 PARTS = HEAD // TAIL
-AHEAD = 4
-BEHIND = 8
-
+FORWARD = 2
+EXPERT = 4
+RETURN = 7
+COMBINE = 10
 
 def iota(shape, dim):
     return lax.broadcasted_iota(jnp.int32, shape, dim)
@@ -32,7 +31,7 @@
     return lax.dot_general(a, b, (dims, ((), ())), preferred_element_type=F32)
 
 
-def moe_kernel(tokens, router, routes, gate_hbm, up_hbm, down_hbm, out, send, recv, back, w_gate, w_up, w_down, acc, place_t, place, gates, rows, hidden, tail_acc, ready, weight_sem, send_sem, recv_sem, ret_sem, back_sem):
+def moe_kernel(tokens, router, routes, gate_hbm, up_hbm, down_hbm, out, mid, send, recv, back_mid, back, w_gate, w_up, w_down, acc, place_t, place, gates, rows, hidden, tail_acc, weight_sem, send_sem, recv_sem, ret_sem, ret_mid_sem, line_sem, mid_sem, line_ret_sem, back_sem):
     tok_count, dim = tokens.shape
     num_exp = router.shape[1]
     top_k = routes.shape[0]
@@ -43,55 +42,79 @@
     at_z, at_y = outer // 4, lax.rem(outer, 4)
     at_x, at_c = line // 2, lax.rem(line, 2)
 
-    def peer(k, sign):
-        m = lax.rem(k * STRIDE, NUM_DEV)
-        to_c = lax.rem(at_c + m, 2)
-        turn = sign * (1 - 2 * FLIP * (at_c if sign > 0 else to_c))
-        shift_x = lax.rem(m // 2, 4)
-        shift_y = lax.rem(m // 8 + MIX * shift_x, 4)
-        shift_z = lax.rem(m // 32 + MIX * shift_x, 4)
-        to_z = lax.rem(at_z + 4 + turn * shift_z, 4)
-        to_y = lax.rem(at_y + 4 + turn * shift_y, 4)
-        to_x = lax.rem(at_x + 4 + turn * shift_x, 4)
-        return {'outer': to_z * 4 + to_y, 'expert': to_x * 2 + to_c}
-
-    def expert_of(k):
-        m = (k * STRIDE) & (NUM_DEV - 1)
-        turn = 1 - 2 * FLIP * at_c
-        shift_x = (m >> 1) & 3
-        to_z = (at_z + turn * ((m >> 5) + MIX * shift_x)) & 3
-        to_y = (at_y + turn * ((m >> 3) + MIX * shift_x)) & 3
-        to_x = (at_x + turn * shift_x) & 3
-        to_c = (at_c + m) & 1
-        return to_z * 32 + to_y * 8 + to_x * 2 + to_c
-
-    def dispatch(k, sign=1):
-        return pltpu.make_async_remote_copy(src_ref=send.at[k], dst_ref=recv.at[k], send_sem=send_sem.at[k], recv_sem=recv_sem.at[k], device_id=peer(k, sign), device_id_type=MESH)
-
-    def give_back(k, sign=-1):
-        return pltpu.make_async_remote_copy(src_ref=recv.at[k], dst_ref=back.at[k], send_sem=ret_sem.at[k], recv_sem=back_sem.at[k], device_id=peer(k, sign), device_id_type=MESH)
-
-    def each(group, what):
+    def line_shift(g):
+        other = g // (2 * 4)
+        n = lax.rem(g // 2 + other, 4)
+        return n + n // 2 - 2 * (n // 3), other
+
+    def line_peer(g, sign):
+        shift_x, shift_c = line_shift(g)
+        return {'outer': outer, 'expert': lax.rem(at_x + 4 + sign * shift_x, 4) * 2 + lax.rem(at_c + shift_c, 2)}
+
+    def outer_at(g, i, sign, core):
+        shift = SHIFTS[i] + lax.rem(g, 2) * (SHIFTS[GROUP + i] - SHIFTS[i])
+        turn = sign * (1 - 2 * core)
+        to_z = lax.rem(at_z + 4 + turn * (shift // 4), 4)
+        to_y = lax.rem(at_y + 4 + turn * lax.rem(shift, 4), 4)
+        return to_z * 4 + to_y
+
+    def plane_peer(g, i, sign):
+        return {'outer': outer_at(g, i, sign, at_c), 'expert': line}
+
+    def experts_of(g, which):
+        shift_x, shift_c = line_shift(g)
+        to_c = lax.rem(at_c + shift_c, 2)
+        to_line = lax.rem(at_x + shift_x, 4) * 2 + to_c
+        found = jnp.zeros_like(which)
+        for i in range(GROUP):
+            found = jnp.where(which == i, outer_at(g, i, 1, to_c) * 8 + to_line, found)
+        return found
+
+    def copy(src, dst, sent, got, where):
+        return pltpu.make_async_remote_copy(src_ref=src, dst_ref=dst, send_sem=sent, recv_sem=got, device_id=where, device_id_type=MESH)
+
+    def span(g, first):
+        return pl.ds(g * GROUP + first, GROUP - first)
+
+    def line_out(g, first):
+        return copy(send.at[span(g, first)], mid.at[span(g, first)], line_sem.at[g], mid_sem.at[g], line_peer(g, 1))
+
+    def line_back(g, first):
+        return copy(back_mid.at[span(g, first)], back.at[span(g, first)], line_ret_sem.at[g], back_sem.at[g], line_peer(g, -1))
+
+    def final_out(k, src, where):
+        return copy(src.at[k], recv.at[k], send_sem.at[k], recv_sem.at[k], where)
+
+    def first_back(k, dst, where):
+        return copy(recv.at[k], dst.at[k], ret_sem.at[k], ret_mid_sem.at[k], where)
+
+    def by_half(g, what):
+        @pl.when(lax.rem(g, 2) == 0)
+        def _():
+            what(1)
+
+        @pl.when(lax.rem(g, 2) == 1)
+        def _():
+            what(0)
+
+    def each(g, what):
         def step(k, carry):
             what(k)
             return carry
 
-        lax.fori_loop(lax.max(group * GROUP, 1), group * GROUP + GROUP, step, 0)
+        lax.fori_loop(lax.max(g * GROUP, 1), g * GROUP + GROUP, step, 0)
 
     lines = lax.axis_size('expert')
     outers = lax.axis_size('outer')
     barrier = pltpu.get_barrier_semaphore()
 
-    def in_line(n):
-        return {'outer': outer, 'expert': lax.rem(line + n, lines)}
-
     for n in range(1, lines):
-        pl.semaphore_signal(barrier, inc=1, device_id=in_line(n), device_id_type=MESH)
+        pl.semaphore_signal(barrier, inc=1, device_id={'outer': outer, 'expert': lax.rem(line + n, lines)}, device_id_type=MESH)
     for n in range(1, outers):
         pl.semaphore_signal(barrier, inc=1, device_id={'outer': lax.rem(outer + n, outers), 'expert': line}, device_id_type=MESH)
     weights = [pltpu.make_async_copy(src, dst, weight_sem.at[n]) for n, (src, dst) in enumerate(((gate_hbm, w_gate), (up_hbm, w_up), (down_hbm, w_down)))]
-    for copy in weights:
-        copy.start()
+    for load in weights:
+        load.start()
 
     kinds = iota((num_exp, tok_count), 0)
     chosen = routes[0:1, :] == kinds
@@ -101,14 +124,11 @@
     earlier = (iota(square, 0) < iota(square, 1)).astype(F32).astype(BF16)
     count = dot(chosen.astype(F32).astype(BF16), earlier)
     place_t[...] = jnp.where(chosen, count, -1.0).astype(BF16)
-    pl.semaphore_wait(barrier, lines + outers - 2)
-    for n in range(1, lines):
-        pl.semaphore_signal(ready, inc=1, device_id=in_line(n), device_id_type=MESH)
 
     def build(g):
         base = g * GROUP
         r = iota((block, num_exp), 0)
-        pick = (expert_of(base + (r >> 4)) == iota((block, num_exp), 1)).astype(F32).astype(BF16)
+        pick = (experts_of(g, r >> 4) == iota((block, num_exp), 1)).astype(F32).astype(BF16)
         slots = dot(pick, place_t[...])
         r = iota((block, tok_count), 0)
         head = (slots == (r & (HEAD - 1)).astype(F32)).astype(F32).astype(BF16)
@@ -128,7 +148,32 @@
         send[pl.ds(base, GROUP), :, dim:] = tail_acc[...].astype(BF16).reshape(GROUP, HEAD, part)
 
     def start_group(g):
-        each(g, lambda k: dispatch(k).start())
+        base = g * GROUP
+
+        def direct(first):
+            for i in range(first, GROUP):
+                final_out(base + i, send, plane_peer(g, i, 1)).start()
+
+        def hop(first):
+            line_out(g, first).start()
+            if first:
+                final_out(base, send, line_peer(g, 1)).start()
+
+        @pl.when(g < 2)
+        def _():
+            by_half(g, direct)
+
+        @pl.when(g >= 2)
+        def _():
+            by_half(g, hop)
+
+    def forward(g):
+        def pass_on(first):
+            line_out(g, first).wait_recv()
+            for i in range(first, GROUP):
+                final_out(g * GROUP + i, mid, plane_peer(g, i, 1)).start()
+
+        by_half(g, pass_on)
 
     def find_gates():
         same = (iota(square, 0) == iota(square, 1)).astype(F32).astype(BF16)
@@ -146,7 +191,7 @@
 
     def run_expert(g):
         base = g * GROUP
-        each(g, lambda k: dispatch(k, -1).wait_recv())
+        each(g, lambda k: final_out(k, send, line_peer(2, 1)).wait_recv())
         rows[0:block, :] = recv[pl.ds(base, GROUP), :, 0:dim].reshape(block, dim)
         tails = recv[pl.ds(base, GROUP), :, dim:].reshape(block, part)
         few = GROUP * TAIL
@@ -181,12 +226,35 @@
         def _():
             back[0] = recv[0]
 
-        each(g, lambda k: give_back(k).start())
+        def give(first, dst):
+            for i in range(first, GROUP):
+                first_back(base + i, dst, plane_peer(g, i, -1)).start()
+
+        def hop(first):
+            if first:
+                first_back(base, back, line_peer(g, -1)).start()
+            give(first, back_mid)
+
+        @pl.when(g < 2)
+        def _():
+            by_half(g, lambda first: give(first, back))
+
+        @pl.when(g >= 2)
+        def _():
+            by_half(g, hop)
+
+    def hand_on(g):
+        def pass_on(first):
+            for i in range(first, GROUP):
+                first_back(g * GROUP + i, back_mid, line_peer(g, -1)).wait_recv()
+            line_back(g, first).start()
+
+        by_half(g, pass_on)
 
     def combine(g):
         base = g * GROUP
         l = iota((num_exp, block), 1)
-        pick = (expert_of(base + (l >> 4)) == iota((num_exp, block), 0)).astype(F32).astype(BF16)
+        pick = (experts_of(g, l >> 4) == iota((num_exp, block), 0)).astype(F32).astype(BF16)
         slots = dot(place[...], pick)
         l = iota((tok_count, block), 1)
         in_head = slots == (l & (HEAD - 1)).astype(F32)
@@ -196,7 +264,20 @@
         heads = jnp.concatenate([jnp.where(in_head, s, 0.0).astype(BF16) for s in spread], axis=0)
         tails = jnp.concatenate([jnp.where(in_tail, s, 0.0).astype(BF16) for s in spread], axis=0)
         which = jnp.concatenate([which] * 3, axis=0)
-        each(g, lambda k: give_back(k, 1).wait_recv())
+
+        @pl.when(g < 2)
+        def _():
+            each(g, lambda k: first_back(k, back, line_peer(2, -1)).wait_recv())
+
+        def arrive(first):
+            line_back(g, first).wait_recv()
+            if first:
+                first_back(base, back, line_peer(g, -1)).wait_recv()
+
+        @pl.when(g >= 2)
+        def _():
+            by_half(g, arrive)
+
 
         def column(q, carry):
             cols = pl.ds(pl.multiple_of(q * part, part), part)
@@ -210,52 +291,61 @@
 
     build(0)
     recv[0] = send[0]
-    pl.semaphore_wait(ready, lines - 1)
+    pl.semaphore_wait(barrier, lines + outers - 2)
     start_group(0)
 
     def step(i, carry):
         @pl.when((i > 0) & (i < NUM_GROUPS))
         def _():
-            @pl.when(i >= AHEAD)
-            def _():
-                each(i - AHEAD, lambda k: dispatch(k).wait_send())
-
             build(i)
             start_group(i)
 
+        @pl.when((i >= FORWARD + 2) & (i < NUM_GROUPS + FORWARD))
+        def _():
+            forward(i - FORWARD)
+
         @pl.when(i == 2)
         def _():
             find_gates()
 
-        @pl.when(i == AHEAD)
-        def _():
-            for copy in weights:
-                copy.wait()
-
-        @pl.when((i >= AHEAD) & (i < NUM_GROUPS + AHEAD))
-        def _():
-            run_expert(i - AHEAD)
-
-        @pl.when(i >= BEHIND)
-        def _():
-            combine(i - BEHIND)
+        @pl.when(i == EXPERT)
+        def _():
+            for load in weights:
+                load.wait()
+
+        @pl.when((i >= EXPERT) & (i < NUM_GROUPS + EXPERT))
+        def _():
+            run_expert(i - EXPERT)
+
+        @pl.when((i >= RETURN + 2) & (i < NUM_GROUPS + RETURN))
+        def _():
+            hand_on(i - RETURN)
+
+        @pl.when(i >= COMBINE)
+        def _():
+            combine(i - COMBINE)
 
         return carry
 
-    lax.fori_loop(0, NUM_GROUPS + BEHIND, step, 0)
+    lax.fori_loop(0, NUM_GROUPS + COMBINE, step, 0)
     out[...] = acc[...].astype(BF16)
 
     def drain(k, carry):
-        give_back(k).wait_send()
+        final_out(k, send, line_peer(2, 1)).wait_send()
+        first_back(k, back, line_peer(2, -1)).wait_send()
         return carry
 
     lax.fori_loop(1, NUM_DEV, drain, 0)
 
-    def drain_send(k, carry):
-        dispatch(k).wait_send()
+    def drain_line(g, carry):
+        def drained(first):
+            line_out(g, first).wait_send()
+            line_back(g, first).wait_send()
+
+        by_half(g, drained)
         return carry
 
-    lax.fori_loop((NUM_GROUPS - AHEAD) * GROUP, NUM_DEV, drain_send, 0)
+    lax.fori_loop(2, NUM_GROUPS, drain_line, 0)
 
 
 def solution(mesh):
@@ -273,10 +363,11 @@
         dma = pltpu.SemaphoreType.DMA
         return pl.pallas_call(
             moe_kernel,
-            out_shape=jax.ShapeDtypeStruct((tok_count, dim), BF16),
+            out_shape=(jax.ShapeDtypeStruct((tok_count, dim), BF16), jax.ShapeDtypeStruct((NUM_DEV, HEAD, width), BF16)),
             in_specs=[vmem, vmem, vmem, hbm, hbm, hbm],
-            out_specs=vmem,
+            out_specs=(vmem, hbm),
             scratch_shapes=[
+                pltpu.VMEM((NUM_DEV, HEAD, width), BF16),
                 pltpu.VMEM((NUM_DEV, HEAD, width), BF16),
                 pltpu.VMEM((NUM_DEV, HEAD, width), BF16),
                 pltpu.VMEM((NUM_DEV, HEAD, width), BF16),
@@ -290,14 +381,17 @@
                 pltpu.VMEM((few, dim), BF16),
                 pltpu.VMEM((few, ff), BF16),
                 pltpu.VMEM((GROUP * HEAD, dim // PARTS), F32),
-                pltpu.SemaphoreType.REGULAR,
                 dma((3,)),
                 dma((NUM_DEV,)),
                 dma((NUM_DEV,)),
                 dma((NUM_DEV,)),
                 dma((NUM_DEV,)),
+                dma((NUM_GROUPS,)),
+                dma((NUM_GROUPS,)),
+                dma((NUM_GROUPS,)),
+                dma((NUM_GROUPS,)),
             ],
             compiler_params=pltpu.CompilerParams(collective_id=0, has_side_effects=True, vmem_limit_bytes=63 * 2**20),
-        )(tokens, w_router, routes.T, w_gate[0], w_up[0], w_down[0])
+        )(tokens, w_router, routes.T, w_gate[0], w_up[0], w_down[0])[0]
 
     return jax.shard_map(per_device, mesh=mesh, in_specs=(row_spec, P(), row_spec, weight_spec, weight_spec, weight_spec), out_specs=row_spec, check_vma=False)

time: 303 us -> 309 us (1.020)
  the two profiles are of different devices: /device:TPU:0 before, /device:TPU:48 now
where the time goes in v4:
time: 309 us
  Pallas kernels  307 us (99%)
    pallas_call x1, Pallas kernels, per_device(): pl.pallas_call(moe_kernel, out_shape=(jax.ShapeDtypeStruct((tok_count, di...  307 us

profile of v4, /device:TPU:48, one launch (start us, length us, event | category | flops | bytes accessed | tf_op | source)
XLA Modules:
  0.0 309.0 jit_solution(2823749346377990709)
XLA Ops:
  0.0 306.7 %shard_map.64 = (bf16[256,2048]{1,0:T(8,128)(2,1)}, bf16[128,16,2560]{2,1,0:T(8,128)(2,1)}) custom-call(bf16[256,2048]{1,0:T(8,128)(2,1)} %tokens.1, bf16[2048,128]{1,0:T(8,128)(2,1)} %router.1, s32[8,256]{1,0:T(8,128)} %bitcast.7, bf16[2048,768]{1,0:T(8,128)(2,1)} %bitcast.4, bf16[2048,768]{1,0:T(8,128)(2,1)} %bitcast.5, bf16[768,2048]{1,0:T(8,128)(2,1)} %bitcast.6), custom_call_target="tpu_custom_call" | custom-call | tf_op jit(solution)/shard_map/pallas_call | solution.py:364
  306.7 2.3 copy.8

commit v5 on v4

--- a/solution.py
+++ b/solution.py
@@ -11,17 +11,17 @@
 BF16 = jnp.bfloat16
 F32 = jnp.float32
 NUM_DEV = 128
-SHIFTS = (0, 1, 4, 3, 12, 5, 15, 2, 8, 7, 13, 6, 9, 14, 11, 10)
+SHIFTS = (0, 10, 13, 7, 15, 5, 8, 2, 14, 4, 6, 12, 11, 1, 9, 3)
 GROUP = 8
 NUM_GROUPS = NUM_DEV // GROUP
 CAPACITY = 20
 HEAD = 16
 TAIL = CAPACITY - HEAD
 PARTS = HEAD // TAIL
-FORWARD = 2
-EXPERT = 4
-RETURN = 7
-COMBINE = 10
+FORWARD = 4
+EXPERT = 6
+RETURN = 8
+COMBINE = 11
 
 def iota(shape, dim):
     return lax.broadcasted_iota(jnp.int32, shape, dim)
@@ -44,8 +44,10 @@
 
     def line_shift(g):
         other = g // (2 * 4)
-        n = lax.rem(g // 2 + other, 4)
-        return n + n // 2 - 2 * (n // 3), other
+        n = lax.rem(g + 2 * other, 8)
+        pair, last = n // 2, lax.rem(n, 2)
+        odd, big = lax.rem(pair, 2), pair // 2
+        return odd * (1 - big) * (1 + 2 * last) + (1 - odd) * big * (3 - 2 * last) + 2 * odd * big, other
 
     def line_peer(g, sign):
         shift_x, shift_c = line_shift(g)

time: 309 us -> 281 us (0.909)
  the two profiles are of different devices: /device:TPU:48 before, /device:TPU:13 now
where the time goes in v5:
time: 281 us; the launch traced here: 280 us
  Pallas kernels  278 us (99%)
    pallas_call x1, Pallas kernels, per_device(): pl.pallas_call(moe_kernel, out_shape=(jax.ShapeDtypeStruct((tok_count, di...  278 us

profile of v5, /device:TPU:13, one launch (start us, length us, event | category | flops | bytes accessed | tf_op | source)
XLA Modules:
  0.0 280.3 jit_solution(11878122942064525206)
XLA Ops:
  0.0 278.0 %shard_map.64 = (bf16[256,2048]{1,0:T(8,128)(2,1)}, bf16[128,16,2560]{2,1,0:T(8,128)(2,1)}) custom-call(bf16[256,2048]{1,0:T(8,128)(2,1)} %tokens.1, bf16[2048,128]{1,0:T(8,128)(2,1)} %router.1, s32[8,256]{1,0:T(8,128)} %bitcast.7, bf16[2048,768]{1,0:T(8,128)(2,1)} %bitcast.4, bf16[2048,768]{1,0:T(8,128)(2,1)} %bitcast.5, bf16[768,2048]{1,0:T(8,128)(2,1)} %bitcast.6), custom_call_target="tpu_custom_call" | custom-call | tf_op jit(solution)/shard_map/pallas_call | solution.py:366
  278.0 2.3 copy.8

commit v6 on v5

--- a/solution.py
+++ b/solution.py
@@ -267,6 +267,20 @@
         tails = jnp.concatenate([jnp.where(in_tail, s, 0.0).astype(BF16) for s in spread], axis=0)
         which = jnp.concatenate([which] * 3, axis=0)
 
+        def drain(k):
+            final_out(k, send, line_peer(2, 1)).wait_send()
+            first_back(k, back, line_peer(2, -1)).wait_send()
+
+        def drain_line(first):
+            line_out(g, first).wait_send()
+            line_back(g, first).wait_send()
+
+        each(g, drain)
+
+        @pl.when(g >= 2)
+        def _():
+            by_half(g, drain_line)
+
         @pl.when(g < 2)
         def _():
             each(g, lambda k: first_back(k, back, line_peer(2, -1)).wait_recv())
@@ -331,23 +345,6 @@
 
     lax.fori_loop(0, NUM_GROUPS + COMBINE, step, 0)
     out[...] = acc[...].astype(BF16)
-
-    def drain(k, carry):
-        final_out(k, send, line_peer(2, 1)).wait_send()
-        first_back(k, back, line_peer(2, -1)).wait_send()
-        return carry
-
-    lax.fori_loop(1, NUM_DEV, drain, 0)
-
-    def drain_line(g, carry):
-        def drained(first):
-            line_out(g, first).wait_send()
-            line_back(g, first).wait_send()
-
-        by_half(g, drained)
-        return carry
-
-    lax.fori_loop(2, NUM_GROUPS, drain_line, 0)
 
 
 def solution(mesh):

time: 281 us -> 281 us (level)
  the two profiles are of different devices: /device:TPU:13 before, /device:TPU:8 now
where the time goes in v6:
time: 281 us
  Pallas kernels  278 us (99%)
    pallas_call x1, Pallas kernels, per_device(): pl.pallas_call(moe_kernel, out_shape=(jax.ShapeDtypeStruct((tok_count, di...  278 us

profile of v6, /device:TPU:8, one launch (start us, length us, event | category | flops | bytes accessed | tf_op | source)
XLA Modules:
  0.0 280.7 jit_solution(9787335602098775717)
XLA Ops:
  0.0 278.4 %shard_map.64 = (bf16[256,2048]{1,0:T(8,128)(2,1)}, bf16[128,16,2560]{2,1,0:T(8,128)(2,1)}) custom-call(bf16[256,2048]{1,0:T(8,128)(2,1)} %tokens.1, bf16[2048,128]{1,0:T(8,128)(2,1)} %router.1, s32[8,256]{1,0:T(8,128)} %bitcast.7, bf16[2048,768]{1,0:T(8,128)(2,1)} %bitcast.4, bf16[2048,768]{1,0:T(8,128)(2,1)} %bitcast.5, bf16[768,2048]{1,0:T(8,128)(2,1)} %bitcast.6), custom_call_target="tpu_custom_call" | custom-call | tf_op jit(solution)/shard_map/pallas_call | solution.py:363
  278.4 2.3 copy.8
